TPU v7x, 256 devices: a whole 4x4x8 slice. The times are simulated.
256 devices in a mesh: spin: 2 (over core), band: 16 (over x, z_hi), grid: 8 (over z_lo, y).
Axes of the slice: x: 4, y: 4, z: 8 (z_hi: 4, z_lo: 2; z = z_hi * 2 + z_lo), core: 2. Of those that a mesh axis runs over, the one named last changes fastest.
Arguments:
- orbitals: bfloat16 [2, 128, 128, 128, 128], P('spin', 'band', 'grid'), may hold values from -0.14941406 to 0.14941406
- partial_bands: int32 [2, 2], P('spin'), may hold values from 0 to 127
- core_density: float32 [128, 128, 128], P('grid'), may hold values from 0.002 to 0.2
Outputs:
- potential: float32 [2, 128, 128, 128], P('spin', 'grid', 'band')
Inputs may be any that keep to these rules, and one draw needn't show every extreme that they name: `partial_bands`: row s holds, for spin s, the first half-occupied band and the count of half-occupied bands; bands past 128 - 1 do not exist.
All inputs are finite; a program needn't handle non-finite values.
Results may differ from a plain program's by a relative error of at most 0.0003.
Values sent between devices are 32-bit elements; how exact they have to be, the bound alone decides.
A program may use at most 128 MiB of HBM per device.

v0:
```python
import math

import jax
import jax.numpy as jnp
from jax import lax
from jax.sharding import PartitionSpec as P

KAPPA = 0.804
MU_X = 0.2195149727645171
BETA = 0.06672455060314922
GAMMA = (1.0 - math.log(2.0)) / math.pi**2
FZ_NORM = 2.0 ** (4.0 / 3.0) - 2.0
FPP_ZERO = 1.709921
EXACT = lax.Precision.HIGHEST


def cut_along(shard, dim, devices):
    shape = shard.shape
    tiles = shard.reshape(*shape[:dim], devices, shape[dim] // devices, *shape[dim + 1 :])
    return jnp.moveaxis(tiles, dim, 0)


def sum_at_owner(shard, axis, dim):
    devices = lax.axis_size(axis)
    tiles = lax.all_to_all(cut_along(shard, dim, devices), axis, 0, 0, tiled=True)
    return jnp.sum(tiles, axis=0)


def swapped(block, axis, stride):
    count = lax.axis_size(axis)
    route = []
    for low in range(count):
        high = low | 1 << stride
        if high != low and high < count:
            route += [(low, high), (high, low)]
    return lax.ppermute(block, axis, route)


def pw_fit(radius, amp, alpha, beta_one, beta_two, beta_three, beta_four):
    root = jnp.sqrt(radius)
    denom = (
        2.0
        * amp
        * (
            beta_one * root
            + beta_two * radius
            + beta_three * radius * root
            + beta_four * radius * radius
        )
    )
    return -2.0 * amp * (1.0 + alpha * radius) * jnp.log(1.0 + 1.0 / denom)


def exchange_part(double, sigma_four):
    kfermi = (3.0 * math.pi**2 * double) ** (1.0 / 3.0)
    scaled = sigma_four / (4.0 * kfermi * kfermi * double * double)
    enhance = 1.0 + KAPPA - KAPPA / (1.0 + MU_X * scaled / KAPPA)
    return -0.75 / math.pi * kfermi * double * enhance


def xc_energy(n_up, n_down, s_uu, s_ud, s_dd):
    exch = 0.5 * (exchange_part(2.0 * n_up, 4.0 * s_uu) + exchange_part(2.0 * n_down, 4.0 * s_dd))
    total = n_up + n_down
    zeta = (n_up - n_down) / total
    radius = (3.0 / (4.0 * math.pi * total)) ** (1.0 / 3.0)
    ec_para = pw_fit(radius, 0.031091, 0.2137, 7.5957, 3.5876, 1.6382, 0.49294)
    ec_ferro = pw_fit(radius, 0.015545, 0.20548, 14.1189, 6.1977, 3.3662, 0.62517)
    neg_stiff = pw_fit(radius, 0.016887, 0.11125, 10.357, 3.6231, 0.88026, 0.49671)
    plus_z = 1.0 + zeta
    minus_z = 1.0 - zeta
    fzeta = (plus_z ** (4.0 / 3.0) + minus_z ** (4.0 / 3.0) - 2.0) / FZ_NORM
    zeta_four = zeta**4
    ec_lda = (
        ec_para
        - neg_stiff * fzeta / FPP_ZERO * (1.0 - zeta_four)
        + (ec_ferro - ec_para) * fzeta * zeta_four
    )
    phi = 0.5 * (plus_z ** (2.0 / 3.0) + minus_z ** (2.0 / 3.0))
    phi_cube = phi * phi * phi
    kfermi = (3.0 * math.pi**2 * total) ** (1.0 / 3.0)
    screen_sq = 4.0 * kfermi / math.pi
    sigma = s_uu + 2.0 * s_ud + s_dd
    tsq = sigma / (4.0 * phi * phi * screen_sq * total * total)
    amp = BETA / GAMMA / (jnp.exp(-ec_lda / (GAMMA * phi_cube)) - 1.0)
    atsq = amp * tsq
    gradient_term = (
        GAMMA
        * phi_cube
        * jnp.log(1.0 + BETA / GAMMA * tsq * (1.0 + atsq) / (1.0 + atsq + atsq * atsq))
    )
    return exch + total * (ec_lda + gradient_term)


def spectral_table(length):
    index = jnp.arange(length, dtype=jnp.int32)
    phase = index[:, None] * index[None, :] % length
    angle = 2.0 * math.pi / length * phase.astype(jnp.float32)
    mode = jnp.where(index < length // 2, index, index - length)
    mode = jnp.where(index == length // 2, 0, mode)
    wave = 2.0 * math.pi / length * mode.astype(jnp.float32)
    sines = jnp.sin(angle)
    cosines = jnp.cos(angle)
    first_term = jnp.dot(sines * wave[None, :], cosines.T, precision=EXACT)
    second_term = jnp.dot(cosines * wave[None, :], sines.T, precision=EXACT)
    return (second_term - first_term) / length


def along_first(stack, table):
    return jnp.einsum("jl,flyz->fjyz", table, stack, precision=EXACT)


def along_second(stack, table):
    return jnp.einsum("jl,fxlz->fxjz", table, stack, precision=EXACT)


def along_third(stack, table):
    return jnp.einsum("fxyl,jl->fxyj", stack, table, precision=EXACT)


def pencil_axes(first, second, third, tables):
    deriv_x = lax.all_to_all(
        along_first(
            lax.all_to_all(first, "grid", split_axis=2, concat_axis=1, tiled=True), tables[0]
        ),
        "grid",
        split_axis=1,
        concat_axis=2,
        tiled=True,
    )
    deriv_y = lax.all_to_all(
        along_second(
            lax.all_to_all(second, "band", split_axis=1, concat_axis=2, tiled=True), tables[1]
        ),
        "band",
        split_axis=2,
        concat_axis=1,
        tiled=True,
    )
    return (deriv_x, deriv_y, along_third(third, tables[2]))


def per_device(orbitals, partial_bands, core_density):
    states = orbitals[0]
    count_local, x_rows, y_cols, z_cells = states.shape
    band_ids = lax.axis_index("band") * count_local + jnp.arange(count_local, dtype=jnp.int32)
    first_band = partial_bands[0, 0]
    span = partial_bands[0, 1]
    weights = jnp.where((band_ids >= first_band) & (band_ids < first_band + span), 0.5, 1.0).astype(
        jnp.float32
    )
    values = states.astype(jnp.float32)
    partial_value = jnp.sum(weights[:, None, None, None] * values * values, axis=0)
    tables = (
        spectral_table(x_rows * lax.axis_size("grid")),
        spectral_table(y_cols),
        spectral_table(z_cells),
    )
    y_block = y_cols // lax.axis_size("band")
    density = sum_at_owner(partial_value, "band", 1)
    core_part = lax.dynamic_slice_in_dim(core_density, lax.axis_index("band") * y_block, y_block, 1)
    own = density + 0.5 * core_part
    other = swapped(own, "spin", 0)
    paired = jnp.stack([own, other])
    deriv_x, deriv_y, deriv_z = pencil_axes(paired, paired, paired, tables)
    steep = jnp.stack([deriv_x[0], deriv_y[0], deriv_z[0]])
    other_steep = jnp.stack([deriv_x[1], deriv_y[1], deriv_z[1]])
    is_up = lax.axis_index("spin") == 0
    dens_up = jnp.where(is_up, own, other)
    dens_down = jnp.where(is_up, other, own)
    grad_up = jnp.where(is_up, steep, other_steep)
    grad_down = jnp.where(is_up, other_steep, steep)
    s_uu = jnp.sum(grad_up * grad_up, axis=0)
    s_ud = jnp.sum(grad_up * grad_down, axis=0)
    s_dd = jnp.sum(grad_down * grad_down, axis=0)
    energy, pull = jax.vjp(xc_energy, dens_up, dens_down, s_uu, s_ud, s_dd)
    derivs = pull(jnp.ones_like(energy))
    dn_own = jnp.where(is_up, derivs[0], derivs[1])
    ds_own = jnp.where(is_up, derivs[2], derivs[4])
    flux = 2.0 * ds_own[None] * steep + derivs[3][None] * other_steep
    div_x, div_y, div_z = pencil_axes(flux[0:1], flux[1:2], flux[2:3], tables)
    potential = dn_own - (div_x[0] + div_y[0] + div_z[0])
    return potential[None]


def solution(mesh):
    in_specs = (P("spin", "band", "grid", None, None), P("spin", None), P("grid", None, None))
    out_specs = P("spin", "grid", "band", None)
    return jax.shard_map(
        per_device, mesh=mesh, in_specs=in_specs, out_specs=out_specs, check_vma=False
    )
```

profile of v0, /device:TPU:8, one launch (start us, length us, event | category | flops | bytes accessed | tf_op | source)
XLA Modules:
  0.0 149.6 jit_solution(3277715592169407252)
XLA Ops:
  0.0 1.3 fusion.126
  2.5 0.6 and_select_fusion
  3.1 3.5 %fusion = f32[16,128,128]{2,1,0:T(8,128)S(1)} fusion(bf16[1,8,16,128,128]{4,3,2,1,0:T(8,128)(2,1)} %param.3, f32[8]{0:T(128)S(1)} %and_select_fusion), kind=kLoop, calls=%fused_computation.1 | loop fusion | flops 8126464 | bytes 5242912 | tf_op jit(solution)/shard_map/reduce_sum | solution.py:152
  6.6 1.1 copy.38
  7.7 11.0 %all-to-all-start = ((f32[16,16,8,128]{3,2,1,0:T(8,128)}), f32[16,16,8,128]{3,2,1,0:T(8,128)S(1)}, u32[]{:S(2)}, u32[]{:S(2)}) async-start(f32[16,16,8,128]{3,2,1,0:T(8,128)} %copy.38), calls=%async_computation | async-start | bytes 2097152 | tf_op jit(solution)/shard_map/all_to_all | solution.py:25
  18.7 30.3 %all-to-all-done = f32[16,16,8,128]{3,2,1,0:T(8,128)S(1)} async-done(((f32[16,16,8,128]{3,2,1,0:T(8,128)}), f32[16,16,8,128]{3,2,1,0:T(8,128)S(1)}, u32[]{:S(2)}, u32[]{:S(2)}) %all-to-all-start) | async-done | bytes 1048608 | tf_op jit(solution)/shard_map/all_to_all | solution.py:25
  49.1 0.1 reduce_sum.46
  49.1 0.9 multiply_add_fusion.6
  50.0 0.1 collective-permute-start
  50.1 1.2 collective-permute-done
  51.3 0.7 copy.39
  52.0 4.9 %all-to-all-start.1 = ((f32[2,16,8,128]{3,1,0,2:T(8,128)}), f32[2,16,8,128]{3,1,0,2:T(8,128)S(1)}, u32[]{:S(2)}, u32[]{:S(2)}) async-start(f32[2,16,8,128]{3,1,0,2:T(8,128)} %copy.39), calls=%async_computation.1 | async-start | bytes 262144 | tf_op jit(solution)/shard_map/all_to_all | solution.py:123
  56.9 0.5 fusion.96
  57.5 0.7 copy.45
  58.1 3.9 %all-to-all-done.1 = f32[2,16,8,128]{3,1,0,2:T(8,128)S(1)} async-done(((f32[2,16,8,128]{3,1,0,2:T(8,128)}), f32[2,16,8,128]{3,1,0,2:T(8,128)S(1)}, u32[]{:S(2)}, u32[]{:S(2)}) %all-to-all-start.1) | async-done | bytes 131104 | tf_op jit(solution)/shard_map/all_to_all | solution.py:123
  62.0 3.5 %all-to-all-start.3 = ((f32[2,16,8,128]{3,2,0,1:T(8,128)}), f32[2,16,8,128]{3,2,0,1:T(8,128)S(1)}, u32[]{:S(2)}, u32[]{:S(2)}) async-start(f32[2,16,8,128]{3,2,0,1:T(8,128)} %copy.45), calls=%async_computation.3 | async-start | bytes 262144 | tf_op jit(solution)/shard_map/all_to_all | solution.py:132
  65.5 0.5 fusion.3
  66.1 0.4 convolution_bitcast_fusion.1
  66.4 0.8 copy.42
  67.2 9.0 %all-to-all-done.3 = f32[2,16,8,128]{3,2,0,1:T(8,128)S(1)} async-done(((f32[2,16,8,128]{3,2,0,1:T(8,128)}), f32[2,16,8,128]{3,2,0,1:T(8,128)S(1)}, u32[]{:S(2)}, u32[]{:S(2)}) %all-to-all-start.3) | async-done | bytes 131104 | tf_op jit(solution)/shard_map/all_to_all | solution.py:132
  76.2 4.7 %all-to-all-start.2 = ((f32[2,128,1,128]{3,0,2,1:T(2,128)}), f32[2,128,1,128]{3,0,2,1:T(2,128)S(1)}, u32[]{:S(2)}, u32[]{:S(2)}) async-start(f32[2,128,1,128]{3,0,2,1:T(2,128)} %copy.42), calls=%async_computation.2 | async-start | bytes 262144 | tf_op jit(solution)/shard_map/all_to_all | solution.py:121
  80.9 0.3 fusion.63
  81.2 0.4 convolution_bitcast_fusion
  81.6 0.8 copy.48
  82.4 3.7 %all-to-all-done.2 = f32[2,128,1,128]{3,0,2,1:T(2,128)S(1)} async-done(((f32[2,128,1,128]{3,0,2,1:T(2,128)}), f32[2,128,1,128]{3,0,2,1:T(2,128)S(1)}, u32[]{:S(2)}, u32[]{:S(2)}) %all-to-all-start.2) | async-done | bytes 131104 | tf_op jit(solution)/shard_map/all_to_all | solution.py:121
  86.0 3.5 %all-to-all-start.4 = ((f32[2,1,128,128]{3,0,1,2:T(2,128)}), f32[2,1,128,128]{3,0,1,2:T(2,128)S(1)}, u32[]{:S(2)}, u32[]{:S(2)}) async-start(f32[2,1,128,128]{3,0,1,2:T(2,128)} %copy.48), calls=%async_computation.4 | async-start | bytes 262144 | tf_op jit(solution)/shard_map/all_to_all | solution.py:130
  89.6 0.1 copy.69
  89.7 10.6 %all-to-all-done.4 = f32[2,1,128,128]{3,0,1,2:T(2,128)S(1)} async-done(((f32[2,1,128,128]{3,0,1,2:T(2,128)}), f32[2,1,128,128]{3,0,1,2:T(2,128)S(1)}, u32[]{:S(2)}, u32[]{:S(2)}) %all-to-all-start.4) | async-done | bytes 131104 | tf_op jit(solution)/shard_map/all_to_all | solution.py:130
  100.3 0.1 fusion.124
  100.4 0.1 multiply_reduce_fusion.1
  100.4 0.8 select_multiply_fusion
  101.3 0.6 fusion.123
  102.0 8.9 %all_to_all.101 = f32[1,16,8,128]{3,1,0,2:T(8,128)S(1)} all-to-all(f32[1,16,8,128]{3,1,0,2:T(8,128)S(1)} %copy.51), channel_id=1, replica_groups=mesh['spin'=2,'band'=16,'grid'=8] {'grid'}, dimensions={2} | all-to-all | bytes 131072 | tf_op jit(solution)/shard_map/all_to_all | solution.py:123
  110.9 3.5 %all-to-all-start.7 = ((f32[1,16,8,128]{3,2,0,1:T(8,128)}), f32[1,16,8,128]{3,2,0,1:T(8,128)S(1)}, u32[]{:S(2)}, u32[]{:S(2)}) async-start(f32[1,16,8,128]{3,2,0,1:T(8,128)} %get-tuple-element.14), calls=%async_computation.7 | async-start | bytes 131072 | tf_op jit(solution)/shard_map/all_to_all | solution.py:132
  114.5 0.3 convolution_bitcast_fusion.3
  114.7 0.7 copy.52
  115.5 9.3 %all-to-all-done.7 = f32[1,16,8,128]{3,2,0,1:T(8,128)S(1)} async-done(((f32[1,16,8,128]{3,2,0,1:T(8,128)}), f32[1,16,8,128]{3,2,0,1:T(8,128)S(1)}, u32[]{:S(2)}, u32[]{:S(2)}) %all-to-all-start.7) | async-done | bytes 65568 | tf_op jit(solution)/shard_map/all_to_all | solution.py:132
  124.8 4.8 %all-to-all-start.6 = ((f32[1,128,1,128]{3,2,0,1:T(1,128)}), f32[1,128,1,128]{3,2,0,1:T(1,128)S(1)}, u32[]{:S(2)}, u32[]{:S(2)}) async-start(f32[1,128,1,128]{3,2,0,1:T(1,128)} %copy.52), calls=%async_computation.6 | async-start | bytes 131072 | tf_op jit(solution)/shard_map/all_to_all | solution.py:121
  129.5 0.3 convolution_bitcast_fusion.2
  129.8 0.1 copy.55
  129.9 4.5 %all-to-all-done.6 = f32[1,128,1,128]{3,2,0,1:T(1,128)S(1)} async-done(((f32[1,128,1,128]{3,2,0,1:T(1,128)}), f32[1,128,1,128]{3,2,0,1:T(1,128)S(1)}, u32[]{:S(2)}, u32[]{:S(2)}) %all-to-all-start.6) | async-done | bytes 65568 | tf_op jit(solution)/shard_map/all_to_all | solution.py:121
  134.5 12.8 %all_to_all.102 = f32[1,1,128,128]{3,1,0,2:T(1,128)S(1)} all-to-all(f32[1,1,128,128]{3,1,0,2:T(1,128)S(1)} %copy.55), channel_id=1, replica_groups=mesh['spin'=2,'band'=16,'grid'=8] {'band'}, dimensions={2} | all-to-all | bytes 131072 | tf_op jit(solution)/shard_map/all_to_all | solution.py:130
  147.2 2.4 %fusion.2 = f32[1,16,8,128]{3,2,1,0:T(8,128)} fusion(f32[3,16,8,128]{3,2,1,0:T(8,128)S(1)} %multiply_add_fusion, f32[16,8,128]{2,1,0:T(8,128)S(1)} %bitcast.101, f32[128,128]{1,0:T(8,128)S(1)} %fusion.3, f32[1,8,16,1,128]{4,2,1,3,0:T(8,128)S(1)} %bitcast.100, f32[16,8,128]{2,1,0:T(8,128)S(1)} %get-tuple-element.10, f32[16,8,128]{2,1,0:T(8,128)S(1)} %get-tuple-element.6, ...), kind=kOutput, calls=%fused_computation.6 | convolution fusion | flops 31539200 | bytes 720897 | tf_op jit(solution)/shard_map/fxyl,jl->fxyj/dot_general | solution.py:117
  (8 shorter events, 0.1 us)
Async XLA Ops:
  7.7 41.4 %all-to-all-start = ((f32[16,16,8,128]{3,2,1,0:T(8,128)}), f32[16,16,8,128]{3,2,1,0:T(8,128)S(1)}, u32[]{:S(2)}, u32[]{:S(2)}) async-start(f32[16,16,8,128]{3,2,1,0:T(8,128)} %copy.38), calls=%async_computation | async-start | bytes 2097152 | tf_op jit(solution)/shard_map/all_to_all | solution.py:25
  50.0 1.3 collective-permute-start
  52.0 10.0 %all-to-all-start.1 = ((f32[2,16,8,128]{3,1,0,2:T(8,128)}), f32[2,16,8,128]{3,1,0,2:T(8,128)S(1)}, u32[]{:S(2)}, u32[]{:S(2)}) async-start(f32[2,16,8,128]{3,1,0,2:T(8,128)} %copy.39), calls=%async_computation.1 | async-start | bytes 262144 | tf_op jit(solution)/shard_map/all_to_all | solution.py:123
  62.0 14.2 %all-to-all-start.3 = ((f32[2,16,8,128]{3,2,0,1:T(8,128)}), f32[2,16,8,128]{3,2,0,1:T(8,128)S(1)}, u32[]{:S(2)}, u32[]{:S(2)}) async-start(f32[2,16,8,128]{3,2,0,1:T(8,128)} %copy.45), calls=%async_computation.3 | async-start | bytes 262144 | tf_op jit(solution)/shard_map/all_to_all | solution.py:132
  76.2 9.8 %all-to-all-start.2 = ((f32[2,128,1,128]{3,0,2,1:T(2,128)}), f32[2,128,1,128]{3,0,2,1:T(2,128)S(1)}, u32[]{:S(2)}, u32[]{:S(2)}) async-start(f32[2,128,1,128]{3,0,2,1:T(2,128)} %copy.42), calls=%async_computation.2 | async-start | bytes 262144 | tf_op jit(solution)/shard_map/all_to_all | solution.py:121
  86.0 14.2 %all-to-all-start.4 = ((f32[2,1,128,128]{3,0,1,2:T(2,128)}), f32[2,1,128,128]{3,0,1,2:T(2,128)S(1)}, u32[]{:S(2)}, u32[]{:S(2)}) async-start(f32[2,1,128,128]{3,0,1,2:T(2,128)} %copy.48), calls=%async_computation.4 | async-start | bytes 262144 | tf_op jit(solution)/shard_map/all_to_all | solution.py:130
  110.9 13.8 %all-to-all-start.7 = ((f32[1,16,8,128]{3,2,0,1:T(8,128)}), f32[1,16,8,128]{3,2,0,1:T(8,128)S(1)}, u32[]{:S(2)}, u32[]{:S(2)}) async-start(f32[1,16,8,128]{3,2,0,1:T(8,128)} %get-tuple-element.14), calls=%async_computation.7 | async-start | bytes 131072 | tf_op jit(solution)/shard_map/all_to_all | solution.py:132
  124.8 9.7 %all-to-all-start.6 = ((f32[1,128,1,128]{3,2,0,1:T(1,128)}), f32[1,128,1,128]{3,2,0,1:T(1,128)S(1)}, u32[]{:S(2)}, u32[]{:S(2)}) async-start(f32[1,128,1,128]{3,2,0,1:T(1,128)} %copy.52), calls=%async_computation.6 | async-start | bytes 131072 | tf_op jit(solution)/shard_map/all_to_all | solution.py:121
where the time goes:
time: 150 us
  waiting for transfers between devices  72.6 us (48%)
  starting transfers between devices  36 us (24%)
  blocking collectives  21.7 us (14%)
  local copies, waits for them, and re-layouts  6.93 us (5%)
  other arithmetic  5.95 us (4%)
  matrix products  5.02 us (3%)
    all_to_all x1, waiting for transfers between devices, sum_at_owner(): lax.all_to_all(cut_along(shard, dim, devices), axis, 0, 0, tiled=True)  30.3 us
    all_to_all x2, waiting for transfers between devices, pencil_axes(): lax.all_to_all(second, 'band', split_axis=1, concat_axis=2, tiled=True)  18.3 us
    all_to_all x1, blocking collectives, pencil_axes(): lax.all_to_all(along_second(lax.all_to_all(second, 'band', split_axis=1,...  12.8 us
    all_to_all x1, starting transfers between devices, sum_at_owner(): lax.all_to_all(cut_along(shard, dim, devices), axis, 0, 0, tiled=True)  11 us
    all_to_all x1, waiting for transfers between devices, pencil_axes(): lax.all_to_all(along_second(lax.all_to_all(second, 'band', split_axis=1,...  10.6 us
    all_to_all x2, starting transfers between devices, pencil_axes(): lax.all_to_all(along_first(lax.all_to_all(first, 'grid', split_axis=2, co...  9.47 us
    all_to_all x1, blocking collectives, pencil_axes(): lax.all_to_all(first, 'grid', split_axis=2, concat_axis=1, tiled=True)  8.94 us
    all_to_all x2, waiting for transfers between devices, pencil_axes(): lax.all_to_all(along_first(lax.all_to_all(first, 'grid', split_axis=2, co...  8.22 us
  transfers between devices with their start and end apart: 8, of which 8 were waited for; matrix products, arithmetic and copies ran while one was open for 4% of the time, Pallas kernels for 0%

commit v1 on v0

v1 whole, which is shorter than its diff:
```python
import math

import jax
import jax.numpy as jnp
import numpy as np
from jax import lax
from jax.experimental import pallas as pl
from jax.experimental.pallas import tpu as pltpu
from jax.sharding import PartitionSpec as P

KAPPA = 0.804
MU_X = 0.2195149727645171
BETA = 0.06672455060314922
GAMMA = (1.0 - math.log(2.0)) / math.pi**2
FZ_NORM = 2.0 ** (4.0 / 3.0) - 2.0
FPP_ZERO = 1.709921

MESH = pl.DeviceIdType.MESH
F32 = jnp.float32
N = 128
XR = 16
NX4 = 4
NZ4 = 4
BAND = NX4 * NZ4
GRID = 8
YB = N // BAND
YQ = N // NX4
CH = 4
CR = XR // CH
HR = CR // 2


def derivative_matrix():
    j = np.arange(N)
    k = j[:, None] - j[None, :]
    ang = np.where(k == 0, 1.0, np.pi * k / N)
    sign = np.where(k % 2 == 0, 1.0, -1.0)
    half = np.pi / N
    return np.where(k == 0, 0.0, half * sign / np.tan(ang)).astype(np.float32)


def pw_fit(r, root, amp, alpha, b1, b2, b3, b4):
    denom = (2.0 * amp) * (root * (b1 + root * (b2 + root * (b3 + root * b4))))
    slope = (2.0 * amp) * (0.5 * b1 / root + (b2 + root * (1.5 * b3 + root * (2.0 * b4))))
    log = jnp.log(1.0 + 1.0 / denom)
    front = (-2.0 * amp) * (1.0 + alpha * r)
    value = front * log
    deriv = (-2.0 * amp * alpha) * log - front * slope / (denom * (denom + 1.0))
    return value, deriv


def cbrt(x):
    return jnp.exp(jnp.log(x) * (1.0 / 3.0))


def xc_derivs(own, other, s_own, s_mix, s_other):
    total = own + other
    inv_n = 1.0 / total
    c_own = cbrt(own)
    c_other = cbrt(other)
    c_tot = cbrt(total)
    inv_c = 1.0 / c_tot
    double = 2.0 * own
    kf = (6.0 * math.pi**2) ** (1.0 / 3.0) * c_own
    inv_kn = 1.0 / (kf * double)
    s2 = s_own * inv_kn * inv_kn
    inv_den = 1.0 / (1.0 + (MU_X / KAPPA) * s2)
    enh = (1.0 + KAPPA) - KAPPA * inv_den
    enh_d = MU_X * inv_den * inv_den
    dn_x = (-1.0 / math.pi) * kf * (enh - 2.0 * s2 * enh_d)
    ds_x = (-3.0 / (8.0 * math.pi)) * enh_d * inv_kn
    two13 = 2.0 ** (1.0 / 3.0)
    plus = double * inv_n
    minus = 2.0 * other * inv_n
    zeta = (own - other) * inv_n
    plus13 = two13 * c_own * inv_c
    minus13 = two13 * c_other * inv_c
    radius = (3.0 / (4.0 * math.pi)) ** (1.0 / 3.0) * inv_c
    root = jnp.sqrt(radius)
    ec0, ec0_r = pw_fit(radius, root, 0.031091, 0.2137, 7.5957, 3.5876, 1.6382, 0.49294)
    ec1, ec1_r = pw_fit(radius, root, 0.015545, 0.20548, 14.1189, 6.1977, 3.3662, 0.62517)
    ac, ac_r = pw_fit(radius, root, 0.016887, 0.11125, 10.357, 3.6231, 0.88026, 0.49671)
    fz = (plus * plus13 + minus * minus13 - 2.0) * (1.0 / FZ_NORM)
    fz_d = (4.0 / 3.0 / FZ_NORM) * (plus13 - minus13)
    z2 = zeta * zeta
    z3 = z2 * zeta
    z4 = z2 * z2
    w1 = (-1.0 / FPP_ZERO) * (1.0 - z4)
    diff = ec1 - ec0
    mix = ac * w1 + diff * z4
    ec = ec0 + fz * mix
    ec_r = ec0_r + fz * (ac_r * w1 + (ec1_r - ec0_r) * z4)
    ec_z = fz_d * mix + 4.0 * z3 * fz * (ac * (1.0 / FPP_ZERO) + diff)
    phi = 0.5 * (plus13 * plus13 + minus13 * minus13)
    phi_d = (1.0 / 3.0) * (1.0 / plus13 - 1.0 / minus13)
    inv_phi = 1.0 / phi
    phi3 = phi * phi * phi
    kf_tot = (3.0 * math.pi**2) ** (1.0 / 3.0)
    tfac = (math.pi / (16.0 * kf_tot)) * inv_phi * inv_phi * inv_c * inv_n * inv_n
    sigma = s_own + 2.0 * s_mix + s_other
    t2 = sigma * tfac
    inv_gp3 = (1.0 / GAMMA) * inv_phi * inv_phi * inv_phi
    ex = jnp.exp(-ec * inv_gp3)
    amp = (BETA / GAMMA) / (ex - 1.0)
    y = amp * t2
    den = 1.0 + y + y * y
    inv_d = 1.0 / den
    ct = (BETA / GAMMA) * t2
    q = ct * (1.0 + y) * inv_d
    grad_h = GAMMA * phi3 * jnp.log(1.0 + q)
    scale = GAMMA * phi3 / (1.0 + q) * inv_d * inv_d
    h_t = scale * ((BETA / GAMMA) * (1.0 + 2.0 * y))
    h_a = -scale * (ct * t2) * (y * (2.0 + y))
    h_ec = h_a * (amp * amp * ex * (GAMMA / BETA) * inv_gp3)
    h_phi = inv_phi * (3.0 * (grad_h - ec * h_ec) - 2.0 * t2 * h_t)
    one_ec = 1.0 + h_ec
    e_n = ec + grad_h - (1.0 / 3.0) * radius * ec_r * one_ec - (7.0 / 3.0) * t2 * h_t
    e_z = ec_z * one_ec + phi_d * h_phi
    dn = dn_x + e_n + e_z * minus
    ds_c = total * h_t * tfac
    return dn, ds_x + ds_c, 2.0 * ds_c


def kernel(
    orb_hbm, bands_ref, core_hbm, dmat_ref, out_ref,
    orb, part, core, x_in, x_out, summed, z_in,
    dens, dens_o, grad, grad_o, flux, turned, x_line, x_res, x_back, y_line, y_res, y_back,
    orb_sem, core_sem, xs_sem, xr_sem, zs_sem, zr_sem, ps_sem, pr_sem, ys_sem, yr_sem, gs_sem, gr_sem,
):
    spin = lax.axis_index("spin")
    band = lax.axis_index("band")
    grid = lax.axis_index("grid")
    bx = band // NZ4
    bz = lax.rem(band, NZ4)
    sends = []

    def at_band(x, z):
        return (spin, lax.rem(x, NX4) * NZ4 + lax.rem(z, NZ4), grid)

    def copy(src, dst, send_sem, recv_sem, device):
        return pltpu.make_async_remote_copy(
            src_ref=src, dst_ref=dst, send_sem=send_sem, recv_sem=recv_sem,
            device_id=device, device_id_type=MESH,
        )

    def send(*args):
        c = copy(*args)
        c.start()
        sends.append(c)

    def arrived(dst, recv_sem):
        copy(dst, dst, recv_sem, recv_sem, (spin, band, grid)).wait_recv()

    order = (2, 1, 3, 0)

    def y_of(r):
        return pl.multiple_of(lax.rem(bx + r, NX4) * YQ, YQ)

    def load(c, r):
        window = (slice(None), pl.ds(c * CR, CR), pl.ds(y_of(r), YQ), slice(None))
        return pltpu.make_async_copy(
            orb_hbm.at[(0, *window)], orb.at[:, pl.ds(c * CR, CR), pl.ds(r * YQ, YQ), :],
            orb_sem.at[c, r],
        )

    for c in range(CH):
        for r in order:
            load(c, r).start()
    y_own = pl.multiple_of(band * YB, YB)
    core_copy = pltpu.make_async_copy(core_hbm.at[:, pl.ds(y_own, YB), :], core, core_sem)
    core_copy.start()

    barrier = pltpu.get_barrier_semaphore()
    peers = [at_band(bx + 1, bz), at_band(bx + 3, bz)]
    peers += [at_band(bx, bz + d) for d in (1, 2, 3)]
    peers += [(spin, band, lax.rem(grid + d, GRID)) for d in range(1, GRID)]
    peers += [(1 - spin, band, grid)]
    for peer in peers:
        pl.semaphore_signal(barrier, inc=1, device_id=peer, device_id_type=MESH)

    first = bands_ref[0, 0]
    last = first + bands_ref[0, 1]
    weights = []
    for b in range(8):
        ident = band * 8 + b
        weights.append(jnp.where((ident >= first) & (ident < last), 0.5, 1.0).astype(F32))

    def density(c, r):
        load(c, r).wait()
        rows, ys = slice(c * CR, (c + 1) * CR), slice(r * YQ, (r + 1) * YQ)
        acc = None
        for b in range(8):
            v = orb[b, rows, ys, :].astype(F32)
            term = weights[b] * (v * v)
            acc = term if acc is None else acc + term
        part[r, rows] = acc

    plus, minus = at_band(bx + 1, bz), at_band(bx + 3, bz)

    def half(c, h):
        return pl.ds(c * CR + h * HR, HR)

    def x_send(stream, c, src):
        target = minus if stream % 2 else plus
        send(src, x_in.at[stream, c], xs_sem.at[stream, c], xr_sem.at[stream, c], target)

    def far(c):
        density(c, 2)
        x_send(0, c, part.at[2, half(c, 0)])
        x_send(1, c, part.at[2, half(c, 1)])

    def direct(c):
        density(c, 1)
        x_send(2, c, part.at[1, half(c, 1)])
        density(c, 3)
        x_send(3, c, part.at[3, half(c, 0)])

    def relay(c):
        for side, r in ((0, 1), (1, 3)):
            arrived(x_in.at[side, c], xr_sem.at[side, c])
            x_out[side, c] = part[r, half(c, side)] + x_in[side, c]
            x_send(4 + side, c, x_out.at[side, c])

    def finish(c):
        density(c, 0)
        for stream in (2, 3, 4, 5):
            arrived(x_in.at[stream, c], xr_sem.at[stream, c])
        summed[half(c, 0)] = part[0, half(c, 0)] + x_in[4, c] + x_in[3, c]
        summed[half(c, 1)] = part[0, half(c, 1)] + x_in[5, c] + x_in[2, c]
        rows = pl.ds(c * CR, CR)
        for d in (2, 1, 3):
            z = lax.rem(bz + d, NZ4)
            ys = pl.ds(pl.multiple_of(z * YB, YB), YB)
            send(
                summed.at[rows, ys, :], z_in.at[d, rows], zs_sem.at[c, d], zr_sem.at[c, d],
                at_band(bx, z),
            )

    far_first = True
    density(0, 2)
    pl.semaphore_wait(barrier, len(peers))
    x_send(0, 0, part.at[2, half(0, 0)])
    x_send(1, 0, part.at[2, half(0, 1)])
    direct(0)
    far(1)
    relay(0)
    for c in range(1, CH):
        direct(c)
        if c + 1 < CH:
            far(c + 1)
        relay(c)
        finish(c - 1)
    finish(CH - 1)

    y_mine = pl.ds(pl.multiple_of(bz * YB, YB), YB)
    core_copy.wait()
    base = summed[:, y_mine, :] + 0.5 * core[...]
    for c in range(CH):
        for d in (1, 2, 3):
            arrived(z_in.at[d, pl.ds(c * CR, CR)], zr_sem.at[c, d])
    own = base + z_in[1] + z_in[2] + z_in[3]
    dens[...] = own.reshape(N, N)

    partner = (1 - spin, band, grid)
    offsets = [(dx, dz) for dx in (2, 1, 3, 0) for dz in (2, 1, 3, 0) if (dx, dz) != (0, 0)]
    g_offsets = (3, 5, 2, 6, 1, 7, 4)

    def dot(a, b):
        return jnp.dot(a, b, precision=lax.Precision.HIGHEST, preferred_element_type=F32)

    def band_rows(b):
        return pl.ds(pl.multiple_of(b * YB, YB), YB)

    def grid_rows(g):
        return pl.ds(pl.multiple_of(g * XR, XR), XR)

    def y_exchange(src, dst, k):
        for dx, dz in offsets:
            d = dx * NZ4 + dz
            p = lax.rem(bx + dx, NX4) * NZ4 + lax.rem(bz + dz, NZ4)
            send(
                src.at[band_rows(p), :], dst.at[band_rows(band), :],
                ys_sem.at[k, d], yr_sem.at[k, d], (spin, p, grid),
            )
        dst[band_rows(band), :] = src[band_rows(band), :]

    def y_wait(dst, k):
        for dx, dz in offsets:
            d = dx * NZ4 + dz
            p = lax.rem(bx + NX4 - dx, NX4) * NZ4 + lax.rem(bz + NZ4 - dz, NZ4)
            arrived(dst.at[band_rows(p), :], yr_sem.at[k, d])

    def x_exchange(src, dst, k):
        for d in g_offsets:
            g = lax.rem(grid + d, GRID)
            send(
                src.at[grid_rows(g), :], dst.at[grid_rows(grid), :],
                gs_sem.at[k, d], gr_sem.at[k, d], (spin, band, g),
            )
        dst[grid_rows(grid), :] = src[grid_rows(grid), :]

    def x_wait(dst, k):
        for d in g_offsets:
            arrived(dst.at[grid_rows(lax.rem(grid + GRID - d, GRID)), :], gr_sem.at[k, d])

    def turn(src, dst):
        for i in range(YB):
            dst[i * XR : (i + 1) * XR, :] = src[pl.ds(i, XR, stride=YB), :]

    def turned_back(ref, xr):
        return ref[pl.ds(xr, YB, stride=XR), :]

    dmat = dmat_ref[...]

    def pencils(y_src, x_src, k):
        y_exchange(y_src, y_line.at[k], 2 * k)
        turn(x_src, turned.at[k])
        x_exchange(turned.at[k], x_line.at[k], 2 * k)

    def lines_x(k):
        x_wait(x_line.at[k], 2 * k)
        x_res[k] = dot(dmat, x_line[k])
        x_exchange(x_res.at[k], x_back.at[k], 2 * k + 1)

    def lines_y(k):
        y_wait(y_line.at[k], 2 * k)
        y_res[k] = dot(dmat, y_line[k])
        y_exchange(y_res.at[k], y_back.at[k], 2 * k + 1)

    pencils(dens, dens, 0)
    send(dens, dens_o, ps_sem.at[0], pr_sem.at[0], partner)
    grad[2] = -dot(dens[...], dmat)
    send(grad.at[2], grad_o.at[2], ps_sem.at[1], pr_sem.at[1], partner)
    lines_x(0)
    lines_y(0)
    x_wait(x_back.at[0], 1)
    for i in range(XR):
        grad[0, i * YB : (i + 1) * YB, :] = turned_back(x_back.at[0], i)
    send(grad.at[0], grad_o.at[0], ps_sem.at[2], pr_sem.at[2], partner)
    y_wait(y_back.at[0], 1)
    send(y_back.at[0], grad_o.at[1], ps_sem.at[3], pr_sem.at[3], partner)
    arrived(dens_o, pr_sem.at[0])
    arrived(grad_o.at[2], pr_sem.at[1])
    arrived(grad_o.at[0], pr_sem.at[2])
    arrived(grad_o.at[1], pr_sem.at[3])

    step = 16
    for i in range(0, N, step):
        rows = slice(i, i + step)
        g = (grad[0, rows, :], y_back[0, rows, :], grad[2, rows, :])
        h = (grad_o[0, rows, :], grad_o[1, rows, :], grad_o[2, rows, :])
        s_own = g[0] * g[0] + g[1] * g[1] + g[2] * g[2]
        s_mix = g[0] * h[0] + g[1] * h[1] + g[2] * h[2]
        s_other = h[0] * h[0] + h[1] * h[1] + h[2] * h[2]
        dn, ds, dm = xc_derivs(dens[rows, :], dens_o[rows, :], s_own, s_mix, s_other)
        for a in range(3):
            flux[a, rows, :] = 2.0 * ds * g[a] + dm * h[a]
        flux[3, rows, :] = dn

    pencils(flux.at[1], flux.at[0], 1)
    flux[3] = flux[3] + dot(flux[2], dmat)
    lines_x(1)
    lines_y(1)
    x_wait(x_back.at[1], 3)
    for i in range(XR):
        rows = slice(i * YB, (i + 1) * YB)
        flux[3, rows, :] = flux[3, rows, :] - turned_back(x_back.at[1], i)
    y_wait(y_back.at[1], 3)
    out_ref[0] = (flux[3] - y_back[1]).reshape(XR, YB, N)
    for c in sends:
        c.wait_send()


def per_device(orbitals, partial_bands, core_density, dmat):
    vm = pltpu.VMEM
    sem = pltpu.SemaphoreType.DMA
    anyspace = pl.BlockSpec(memory_space=pl.ANY)
    return pl.pallas_call(
        kernel,
        out_shape=jax.ShapeDtypeStruct((1, XR, YB, N), F32),
        in_specs=[
            anyspace,
            pl.BlockSpec(memory_space=pltpu.SMEM),
            anyspace,
            pl.BlockSpec(memory_space=pltpu.VMEM),
        ],
        out_specs=pl.BlockSpec(memory_space=pltpu.VMEM),
        scratch_shapes=[
            vm((8, XR, N, N), jnp.bfloat16),
            vm((NX4, XR, YQ, N), F32),
            vm((XR, YB, N), F32),
            vm((6, CH, HR, YQ, N), F32),
            vm((2, CH, HR, YQ, N), F32),
            vm((XR, YQ, N), F32),
            vm((NZ4, XR, YB, N), F32),
            vm((N, N), F32),
            vm((N, N), F32),
            vm((3, N, N), F32),
            vm((3, N, N), F32),
            vm((4, N, N), F32),
            vm((2, N, N), F32),
            vm((2, N, N), F32),
            vm((2, N, N), F32),
            vm((2, N, N), F32),
            vm((2, N, N), F32),
            vm((2, N, N), F32),
            vm((2, N, N), F32),
            sem((CH, NX4)),
            sem,
            sem((6, CH)),
            sem((6, CH)),
            sem((CH, NZ4)),
            sem((CH, NZ4)),
            sem((4,)),
            sem((4,)),
            sem((4, BAND)),
            sem((4, BAND)),
            sem((4, GRID)),
            sem((4, GRID)),
        ],
        compiler_params=pltpu.CompilerParams(collective_id=0, has_side_effects=True),
    )(orbitals, partial_bands, core_density, dmat)


def solution(mesh):
    in_specs = (P("spin", "band", "grid", None, None), P("spin", None), P("grid", None, None))
    out_specs = P("spin", "grid", "band", None)

    def step(orbitals, partial_bands, core_density):
        dmat = jnp.asarray(derivative_matrix())
        return jax.shard_map(
            per_device, mesh=mesh, in_specs=(*in_specs, P(None, None)), out_specs=out_specs,
            check_vma=False,
        )(orbitals, partial_bands, core_density, dmat)

    return step
```

time: 150 us -> 60.5 us (0.40)
  the two profiles are of different devices: /device:TPU:8 before, /device:TPU:1 now
where the time goes in v1:
time: 60.5 us; the launch traced here: 60.3 us
  Pallas kernels  58.8 us (97%)
  local copies, waits for them, and re-layouts  1.47 us (2%)
    pallas_call x1, Pallas kernels, per_device(): pl.pallas_call(kernel, out_shape=jax.ShapeDtypeStruct((1, XR, YB, N), F32...  58.8 us
    unnamed x1, local copies, waits for them, and re-layouts  1.47 us

profile of v1, /device:TPU:1, one launch (start us, length us, event | category | flops | bytes accessed | tf_op | source)
XLA Modules:
  0.0 60.3 jit_solution(5520181617819691579)
XLA Ops:
  0.0 58.8 %shard_map.46 = f32[1,16,8,128]{3,2,1,0:T(8,128)} custom-call(bf16[1,8,16,128,128]{4,3,2,1,0:T(8,128)(2,1)} %orb_hbm.1, s32[1,2]{1,0:T(1,128)} %bands_ref.1, f32[16,128,128]{2,1,0:T(8,128)} %core_hbm.1, f32[128,128]{1,0:T(8,128)} %constant.2.clone.dmat_ref), custom_call_target="tpu_custom_call" | custom-call | tf_op jit(solution)/shard_map/pallas_call | solution.py:378
  58.8 1.5 %copy.6 = f32[1,16,8,128]{3,2,1,0:T(8,128)} copy(f32[1,16,8,128]{3,2,1,0:T(8,128)} %shard_map.46) | data formatting | bytes 131072
